TPU v7x, 256 devices: a whole 4x4x8 slice. The times are simulated.
256 devices in a mesh: order: 16 (over z, core), blk: 16 (over x, y).
Axes of the slice: x: 4, y: 4, z: 8, core: 2. Of those that a mesh axis runs over, the one named last changes fastest.
Arguments:
- latent: bfloat16 [2, 16, 2048, 2048], P(None, None, 'order', 'blk'), may hold values from -0.1875 to 0.1875
- legendre: bfloat16 [2048, 2048, 256], P('order', 'blk'), may hold values from -0.125 to 0.125
- counts: int32 [256, 16, 4096], P(('blk', 'order')), may hold values from 0 to 7
- exposure: float32 [256, 4096], P(('blk', 'order')), may hold values from 0.25 to 4
- slot_order: int32 [2048], replicated, may hold values from 0 to 2047, each once
Outputs:
- gradient: float32 [2, 16, 2048, 2048], P(None, None, 'order', 'blk')
Inputs may be any that keep to these rules, and one draw needn't show every extreme that they name: Slot s holds order slot_order[s]; every order from 0 to 2047 is held by exactly one slot.
All inputs are finite; a program needn't handle non-finite values.
Results may differ from a plain program's by a relative error of at most 0.005.
Values may be sent and summed in bfloat16 or wider, within the bound.
A program may use at most 64 MiB of HBM per device.

v0:
```python
import functools
import math

import jax
import jax.numpy as jnp
from jax import lax
from jax.sharding import Mesh
from jax.sharding import PartitionSpec as P

BLK = ("blk_0", "blk_1")
ORDER = ("order_0", "order_1")
ORDER_BLK = ("order_0", "order_1", "blk_0", "blk_1")
BLK_ORDER = ("blk_0", "blk_1", "order_0", "order_1")


def by_axis(array, axes):
    return functools.reduce(lax.psum, axes, array)


def own_rows(subtotal, axes):
    for axis in axes:
        subtotal = lax.psum_scatter(subtotal, axis, scatter_dimension=0, tiled=True)
    return subtotal


def joined_along(pieces, dim):
    dims = list(pieces.shape[1:])
    dims[dim] *= pieces.shape[0]
    return jnp.moveaxis(pieces, 0, dim).reshape(dims)


def work_in_pieces(array, axis, dim, work, out_dim):
    extent = array.shape[dim]
    pieces = jnp.split(array, 2, axis=dim) if extent % 2 == 0 else [array]
    leading = jnp.arange(lax.axis_size(axis)) * extent
    blocks = [lax.all_gather(share, axis) for share in pieces]
    made = [jax.vmap(work)(b, leading + k * (extent // len(pieces))) for k, b in enumerate(blocks)]
    return joined_along(jnp.concatenate(made, axis=out_dim + 1), out_dim)


def from_everyone(array, axis):
    copies = jnp.broadcast_to(array, (lax.axis_size(axis), *array.shape))
    return lax.all_to_all(copies, axis, split_axis=0, concat_axis=0, tiled=True)


def gathered_copies(array, axis, dim):
    pieces = from_everyone(array, axis)
    return joined_along(pieces, dim)


def trig_table(orders, longitudes):
    column = lax.iota(jnp.int32, longitudes)
    phases = orders[:, None] * column[None, :] % longitudes
    angles = phases.astype(jnp.float32) * (2.0 * math.pi / longitudes)
    weight = jnp.where(orders == 0, 1.0, 2.0).astype(jnp.float32)[:, None]
    return jnp.stack([weight * jnp.cos(angles), -weight * jnp.sin(angles)])


def intensity_residual(field_rows, counts, exposure, cycle_count):
    cycle_sub = field_rows.shape[0]
    first_cycle = (lax.axis_index(BLK) * lax.axis_size(ORDER) + lax.axis_index(ORDER)) * cycle_sub
    cycle_index = first_cycle + lax.iota(jnp.int32, cycle_sub)
    cycle_area = jnp.sin(jnp.pi * (cycle_index.astype(jnp.float32) + 0.5) / cycle_count)
    weight_map = cycle_area[:, None] * exposure
    growth = weight_map[:, None, :] * jnp.exp(field_rows)
    observed = counts.astype(jnp.float32)
    total_growth, total_counts = (
        by_axis(jnp.sum(growth, axis=(0, 2)), ORDER_BLK),
        by_axis(jnp.sum(observed, axis=(0, 2)), ORDER_BLK),
    )
    intensity = growth * (total_counts / total_growth)[None, :, None]
    return ((intensity - observed) * (1.0 / math.sqrt(field_rows.shape[2]))).astype(jnp.bfloat16)


def body(latent, legendre, counts, exposure, slot_order):
    slot_count = legendre.shape[0]
    degrees = legendre.shape[1]
    cycle_count = legendre.shape[2]
    longitudes = counts.shape[2]
    orders_here = lax.dynamic_slice_in_dim(
        slot_order, lax.axis_index(ORDER) * slot_count, slot_count
    )
    degree = lax.axis_index(BLK) * degrees + lax.iota(jnp.int32, degrees)
    nonzero = degree[None, :] >= orders_here[:, None]
    masked = jnp.where(nonzero[None, None], latent, jnp.zeros((), latent.dtype))
    basis = legendre
    spectra = own_rows(
        jnp.einsum("pcsl,slr->rpcs", masked, basis, preferred_element_type=jnp.float32), BLK
    ).astype(jnp.bfloat16)
    cosines = trig_table(orders_here, longitudes)
    rows_here = spectra.astype(jnp.float32)
    field_rows = lax.psum_scatter(
        jnp.einsum("npcs,psj->ncj", rows_here, cosines, precision=lax.Precision.HIGHEST),
        ORDER,
        scatter_dimension=0,
        tiled=True,
    )
    residual = intensity_residual(field_rows, counts, exposure, cycle_count)

    def partial_adjoint(portion, offset):
        return jnp.einsum(
            "ncj,psj->npcs", portion.astype(jnp.float32), cosines, precision=lax.Precision.HIGHEST
        ).astype(jnp.bfloat16)

    returned = work_in_pieces(residual, ORDER, 0, partial_adjoint, 0)
    basis = legendre
    gradient = jnp.einsum(
        "rpcs,slr->pcsl",
        gathered_copies(returned, BLK, 0),
        basis,
        preferred_element_type=jnp.float32,
    )
    return jnp.where(nonzero[None, None], gradient, jnp.zeros((), jnp.float32))


def solution(mesh):
    finer = Mesh(mesh.devices.reshape(8, 2, 4, 4), ("order_0", "order_1", "blk_0", "blk_1"))
    return jax.shard_map(
        body,
        mesh=finer,
        in_specs=(
            P(None, None, ORDER, BLK),
            P(ORDER, BLK, None),
            P(BLK_ORDER, None, None),
            P(BLK_ORDER, None),
            P(),
        ),
        out_specs=P(None, None, ORDER, BLK),
        check_vma=False,
    )
```

profile of v0, /device:TPU:1, one launch (start us, length us, event | category | flops | bytes accessed | tf_op | source)
XLA Modules:
  0.0 305.4 jit_solution(2678399236588692242)
XLA Ops:
  6.5 0.0 reduce-scatter.4.cloned.1.call-start
  6.5 0.8 compare_select_fusion
  7.3 0.1 broadcast_compare_fusion
  7.4 1.3 broadcast_select_fusion
  8.7 6.7 %fusion.7 = f32[256,2,16,128]{0,2,1,3:T(8,128)} fusion(bf16[128,128,256]{2,1,0:T(8,128)(2,1)} %param.6, bf16[2,16,128,128]{3,2,1,0:T(8,128)(2,1)S(1)} %broadcast_select_fusion), kind=kOutput, calls=%fused_computation.12 | convolution fusion | flops 268435456 | bytes 13631488 | tf_op jit(solution)/shard_map/pcsl,slr->rpcs/dot_general | solution.py:88
  15.4 6.0 %copy.17 = f32[256,2,16,128]{3,2,1,0:T(8,128)} copy(f32[256,2,16,128]{0,2,1,3:T(8,128)} %fusion.7) | data formatting | bytes 8388608 | tf_op jit(solution)/shard_map/pcsl,slr->rpcs/transpose | solution.py:88
  21.3 0.0 reduce-scatter.4.cloned.1.call-update
  21.3 0.0 reduce-scatter.6.cloned.1.call-start
  21.4 53.2 %reduce-scatter.4.cloned.1.call-done = f32[64,2,16,128]{3,2,1,0:T(8,128)} async-done(((f32[256,2,16,128]{3,2,1,0:T(8,128)}), f32[64,2,16,128]{3,2,1,0:T(8,128)}) %reduce-scatter.4.cloned.1.call-update) | async-done | bytes 1048592 | tf_op jit(solution)/shard_map/reduce_scatter | solution.py:22
  74.6 0.0 reduce-scatter.6.cloned.1.call-update
  74.6 0.0 reduce-scatter.8.cloned.1.call-start
  74.7 9.8 %cosine_multiply_fusion = (f32[1,128,4096]{2,1,0:T(8,128)S(1)}, f32[1,128,4096]{2,1,0:T(8,128)}) fusion(s32[128]{0:T(128)S(1)} %get-tuple-element.14, f32[128]{0:T(128)S(1)} %get-tuple-element.13, f32[128]{0:T(128)S(1)} %fusion.34), kind=kLoop, calls=%fused_computation.19 | loop fusion | flops 8388608 | bytes 4195840 | tf_op jit(solution)/shard_map/mul | solution.py:56
  84.4 17.4 %reduce-scatter.6.cloned.1.call-done = f32[16,2,16,128]{3,2,1,0:T(8,128)} async-done(((f32[64,2,16,128]{3,2,1,0:T(8,128)}), f32[16,2,16,128]{3,2,1,0:T(8,128)}) %reduce-scatter.6.cloned.1.call-update) | async-done | bytes 262160 | tf_op jit(solution)/shard_map/reduce_scatter | solution.py:22
  101.8 5.9 %convolution_bitcast_fusion = f32[16,16,4096]{2,1,0:T(8,128)} fusion(f32[1,128,4096]{2,1,0:T(8,128)} %get-tuple-element.16, f32[1,128,4096]{2,1,0:T(8,128)S(1)} %get-tuple-element.15, f32[16,2,16,128]{3,2,1,0:T(8,128)} %reduce-scatter.6.cloned.1.call-done), kind=kOutput, calls=%fused_computation.4 | convolution fusion | flops 3222339584 | bytes 8650752 | tf_op jit(solution)/shard_map/npcs,psj->ncj/dot_general | solution.py:93
  107.7 0.0 copy-start
  107.8 0.0 copy-start.1
  107.8 0.0 reduce-scatter.8.cloned.1.call-update
  107.8 0.0 all-gather.3.cloned.1.call-start
  107.9 0.8 copy-done
  108.7 0.1 convert_reduce_fusion
  108.8 0.0 copy-done.1
  108.9 60.5 %reduce-scatter.8.cloned.1.call-done = f32[1,16,4096]{2,1,0:T(8,128)} async-done(((f32[16,16,4096]{2,1,0:T(8,128)}), f32[1,16,4096]{2,1,0:T(8,128)}) %reduce-scatter.8.cloned.1.call-update) | async-done | bytes 262160 | tf_op jit(solution)/shard_map/reduce_scatter | solution.py:92
  169.4 1.1 fusion.30
  170.5 15.0 %all-reduce = (f32[16]{0:T(128)S(1)}, f32[16]{0:T(128)S(1)}) all-reduce(f32[16]{0:T(128)S(1)} %convert_reduce_fusion, f32[16]{0:T(128)S(1)} %fusion.30), channel_id=1, replica_groups=mesh['order_0'=8,'order_1'=2,'blk_0'=4,'blk_1'=4] {'order_0'}, use_global_device_ids=true, to_apply=%region_4.5 | all-reduce | flops 32 | bytes 256 | tf_op jit(solution)/shard_map/psum | solution.py:17
  185.5 5.0 %all-reduce.3 = (f32[16]{0:T(128)S(1)}, f32[16]{0:T(128)S(1)}) all-reduce(f32[16]{0:T(128)S(1)} %get-tuple-element.5, f32[16]{0:T(128)S(1)} %get-tuple-element.6), channel_id=1, replica_groups=mesh['order_0'=8,'order_1'=2,'blk_0'=4,'blk_1'=4] {'order_1'}, use_global_device_ids=true, to_apply=%region_5.6 | all-reduce | flops 32 | bytes 256 | tf_op jit(solution)/shard_map/psum | solution.py:17
  190.5 8.3 %all-reduce.2 = (f32[16]{0:T(128)S(1)}, f32[16]{0:T(128)S(1)}) all-reduce(f32[16]{0:T(128)S(1)} %get-tuple-element.11, f32[16]{0:T(128)S(1)} %get-tuple-element.12), channel_id=1, replica_groups=mesh['order_0'=8,'order_1'=2,'blk_0'=4,'blk_1'=4] {'blk_0'}, use_global_device_ids=true, to_apply=%region_6.7 | all-reduce | flops 32 | bytes 256 | tf_op jit(solution)/shard_map/psum | solution.py:17
  198.8 8.5 %all-reduce.1 = (f32[16]{0:T(128)S(1)}, f32[16]{0:T(128)S(1)}) all-reduce(f32[16]{0:T(128)S(1)} %get-tuple-element.9, f32[16]{0:T(128)S(1)} %get-tuple-element.10), channel_id=1, replica_groups=mesh['order_0'=8,'order_1'=2,'blk_0'=4,'blk_1'=4] {'blk_1'}, use_global_device_ids=true, to_apply=%region_7.8 | all-reduce | flops 32 | bytes 256 | tf_op jit(solution)/shard_map/psum | solution.py:17
  207.3 1.7 multiply_convert_fusion
  209.0 0.0 all-gather.3.cloned.1.call-update
  209.0 38.5 %all-gather.3.cloned.1.call-done = bf16[16,16,4096]{2,1,0:T(8,128)(2,1)} async-done(((bf16[1,16,4096]{2,1,0:T(8,128)(2,1)}), bf16[16,16,4096]{2,1,0:T(8,128)(2,1)}) %all-gather.3.cloned.1.call-update) | async-done | bytes 2097168 | tf_op jit(solution)/shard_map/all_gather | solution.py:36
  247.5 4.4 %fusion.24 = bf16[16,2,16,128]{3,2,0,1:T(8,128)(2,1)S(1)} fusion(bf16[16,16,4096]{2,1,0:T(8,128)(2,1)} %all-gather.3.cloned.1.call-done, f32[1,128,4096]{2,1,0:T(8,128)} %get-tuple-element.16, f32[1,128,4096]{2,1,0:T(8,128)S(1)} %get-tuple-element.15), kind=kOutput, calls=%fused_computation.24 | convolution fusion | flops 3222339584 | bytes 6422528 | tf_op jit(solution)/shard_map/vmap(ncj,psj->npcs)/dot_general | solution.py:101
  251.9 0.4 broadcast_in_dim.50
  252.3 33.5 %all_to_all.5 = bf16[16,16,2,16,128]{4,3,2,1,0:T(8,128)(2,1)S(1)} all-to-all(bf16[16,16,2,16,128]{4,3,2,1,0:T(8,128)(2,1)S(1)} %broadcast_in_dim.50), channel_id=1, replica_groups=mesh['order_0'=8,'order_1'=2,'blk_0'=4,'blk_1'=4] {'blk_0','blk_1'}, dimensions={0} | all-to-all | bytes 4194304 | tf_op jit(solution)/shard_map/all_to_all | solution.py:43
  285.9 3.4 %copy.19 = bf16[256,2,16,128]{0,2,1,3:T(8,128)(2,1)} copy(bf16[256,2,16,128]{3,2,1,0:T(8,128)(2,1)S(1)} %bitcast.45) | data formatting | bytes 4194304 | tf_op jit(solution)/shard_map/reshape | solution.py:29
  289.3 7.0 %select_bitcast_fusion = f32[2,16,128,128]{3,1,0,2:T(8,128)S(1)} fusion(bf16[256,2,16,128]{0,2,1,3:T(8,128)(2,1)} %copy.19, bf16[128,128,256]{2,1,0:T(8,128)(2,1)} %param.6, pred[128,128]{1,0:T(8,128)(4,1)S(1)} %broadcast_compare_fusion), kind=kOutput, calls=%fused_computation.17 | convolution fusion | flops 268959744 | bytes 12599296 | tf_op jit(solution)/shard_map/rpcs,slr->pcsl/dot_general | solution.py:107
  296.3 2.6 copy.20
  (5 shorter events, 0.0 us)
Async XLA Ops:
  6.5 68.0 %reduce-scatter.4.cloned.1.call-start = ((), (), s32[]{:S(2)}) async-start(), calls=%async_computation.4 | async-start | bytes 5242880 | tf_op jit(solution)/shard_map/reduce_scatter | solution.py:22
  21.3 80.5 %reduce-scatter.6.cloned.1.call-start = ((), (), s32[]{:S(2)}) async-start(), calls=%async_computation.5 | async-start | bytes 1310720 | tf_op jit(solution)/shard_map/reduce_scatter | solution.py:22
  74.6 94.8 %reduce-scatter.8.cloned.1.call-start = ((), (), s32[]{:S(2)}) async-start(), calls=%async_computation.6 | async-start | bytes 4456448 | tf_op jit(solution)/shard_map/reduce_scatter | solution.py:92
  107.7 0.9 copy-start
  107.8 1.1 copy-start.1
  107.8 139.7 %all-gather.3.cloned.1.call-start = ((), (), s32[]{:S(2)}) async-start(), calls=%async_computation.7 | async-start | bytes 2228224 | tf_op jit(solution)/shard_map/all_gather | solution.py:36
Sparse Core Ops, SparseCore 0:
  21.5 53.0 reduce-scatter.3
  77.1 24.6 reduce-scatter.5
  107.9 61.4 reduce-scatter.7
  209.2 38.2 all-gather.2
where the time goes:
time: 306 us; the launch traced here: 305 us
  waiting for transfers between devices  170 us (56%)
  blocking collectives  70.3 us (23%)
  matrix products  23.9 us (8%)
  other arithmetic  14.9 us (5%)
  between operations  13.3 us (4%)
  local copies, waits for them, and re-layouts  13.1 us (4%)
    reduce_scatter x2, waiting for transfers between devices, own_rows(): subtotal = lax.psum_scatter(subtotal, axis, scatter_dimension=0, tiled=True)  70.6 us
    reduce_scatter x1, waiting for transfers between devices, body(): lax.psum_scatter(jnp.einsum('npcs,psj->ncj', rows_here, cosines, precisio...  60.5 us
    all_gather x1, waiting for transfers between devices, work_in_pieces(): blocks = [lax.all_gather(share, axis) for share in pieces]  38.5 us
    psum x4, blocking collectives, by_axis(): return functools.reduce(lax.psum, axes, array)  36.8 us
    all_to_all x1, blocking collectives, from_everyone(): return lax.all_to_all(copies, axis, split_axis=0, concat_axis=0, tiled=True)  33.5 us
    mul x1, other arithmetic, trig_table(): return jnp.stack([weight * jnp.cos(angles), -weight * jnp.sin(angles)])  9.75 us
    dot_general x1, matrix products, body(): jnp.einsum('rpcs,slr->pcsl', gathered_copies(returned, BLK, 0), basis, pr...  6.98 us
    dot_general x1, matrix products, body(): jnp.einsum('pcsl,slr->rpcs', masked, basis, preferred_element_type=jnp.fl...  6.68 us
  transfers between devices with their start and end apart: 4, of which 4 were waited for; matrix products, arithmetic and copies ran while one was open for 3% of the time, Pallas kernels for 0%

commit v1 on v0

v1 whole, which is shorter than its diff:
```python
import functools
import math

import jax
import jax.numpy as jnp
import numpy as np
from jax import lax
from jax.experimental import pallas as pl
from jax.experimental.pallas import tpu as pltpu
from jax.sharding import Mesh
from jax.sharding import PartitionSpec as P

BLK = ("blk_0", "blk_1")
ORDER = ("order_0", "order_1")
BLK_ORDER = ("blk_0", "blk_1", "order_0", "order_1")
AXES = ("order_0", "order_1", "blk_0", "blk_1")
MESH = pl.DeviceIdType.MESH
F32 = jnp.float32
BF16 = jnp.bfloat16

GROUP = 16


def hi_lo(x):
    hi = x.astype(BF16)
    return hi, (x - hi.astype(F32)).astype(BF16)


def dot(a, b):
    return jnp.dot(a, b, preferred_element_type=F32)


def np_hi_lo(x):
    x = np.asarray(x, np.float32)
    hi = x.astype(jnp.bfloat16)
    lo = (x - hi.astype(np.float32)).astype(jnp.bfloat16)
    return hi, lo


@functools.cache
def tables():
    a = np.arange(64)
    b = np.arange(32)
    j0 = np.arange(32)
    j1 = np.arange(128)
    turn = 2.0 * np.pi
    aj = turn * ((a[:, None] * j1[None, :]) % 128) / 128.0
    bj0 = turn * ((b[:, None] * j0[None, :]) % 32) / 32.0
    bj1 = turn * ((b[:, None] * j1[None, :]) % 4096) / 4096.0
    first = np.zeros((2, 64, 2, 2, 128))
    last = np.zeros((2, 2, 128, 2, 2, 64))
    for b2 in range(2):
        first[b2, :, b2, 0] = np.cos(aj)
        first[b2, :, b2, 1] = np.sin(aj)
        last[b2, 0, :, 0, b2] = np.cos(aj).T
        last[b2, 1, :, 0, b2] = np.sin(aj).T
        last[b2, 0, :, 1, b2] = -np.sin(aj).T
        last[b2, 1, :, 1, b2] = np.cos(aj).T
    fh, fl = np_hi_lo(first.reshape(128, 512))
    t1 = np.concatenate([fh, fl], axis=0)
    lh, ll = np_hi_lo(last.reshape(512, 256))
    t4 = np.concatenate([lh, ll], axis=0)
    w3 = np.concatenate([np.cos(bj0).T, -np.sin(bj0).T], axis=1)
    wh, wl = np_hi_lo(w3)
    w3 = np.concatenate([wh, wl, wh], axis=1)
    b_of = np.array([2 * b1 + b2 for b2 in range(2) for b1 in range(16)])
    v = np.concatenate([np.cos(bj0)[b_of], -np.sin(bj0)[b_of]], axis=0)
    vh, vl = np_hi_lo(v)
    w3b = np.concatenate([vh, vl, vh], axis=1)
    tw = np.concatenate([np.cos(bj1), np.sin(bj1)], axis=0).astype(np.float32)
    twb = np.concatenate([np.cos(bj1)[b_of], np.sin(bj1)[b_of]], axis=0).astype(np.float32)
    return t1, t4, w3, w3b, tw, twb


def spectra_kernel(lat_ref, leg_ref, out_ref, acc):
    g = pl.program_id(0)
    for i in range(GROUP):
        res = dot(lat_ref[i], leg_ref[i])
        row = g * GROUP + i
        acc[0, pl.ds(row, 32, stride=128), :] = res[:, :128]
        acc[1, pl.ds(row, 32, stride=128), :] = res[:, 128:]

    @pl.when(g == pl.num_programs(0) - 1)
    def _():
        def step(pc, _):
            for t in range(2):
                tile = acc[t, pl.ds(pl.multiple_of(pc * 128, 128), 128), :].T.astype(BF16)
                for q in range(8):
                    e = 8 * t + q
                    out_ref[e // 4, e % 4, pc] = tile[16 * q : 16 * q + 16]
            return 0

        lax.fori_loop(0, 32, step, 0)


def partial_spectra(lat, leg):
    return pl.pallas_call(
        spectra_kernel,
        grid=(128 // GROUP,),
        out_shape=jax.ShapeDtypeStruct((4, 4, 32, 16, 128), BF16),
        in_specs=[
            pl.BlockSpec((GROUP, 32, 128), lambda g: (g, 0, 0)),
            pl.BlockSpec((GROUP, 128, 256), lambda g: (g, 0, 0)),
        ],
        out_specs=pl.BlockSpec((4, 4, 32, 16, 128), lambda g: (0, 0, 0, 0, 0)),
        scratch_shapes=[pltpu.VMEM((2, 4096, 128), F32)],
        compiler_params=pltpu.CompilerParams(vmem_limit_bytes=40 * 2**20),
    )(lat, leg)


def gradient_kernel(first_degree_ref, order_ref, ret_ref, leg_ref, out_ref, acc):
    g = pl.program_id(0)

    @pl.when(g == 0)
    def _():
        def step(pc, _):
            for t in range(2):
                rows = [ret_ref[(8 * t + q) // 4, (8 * t + q) % 4, pc] for q in range(8)]
                tile = jnp.concatenate(rows, axis=0).astype(F32).T
                acc[t, pl.ds(pl.multiple_of(pc * 128, 128), 128), :] = tile
            return 0

        lax.fori_loop(0, 32, step, 0)

    degree = first_degree_ref[0] + lax.broadcasted_iota(jnp.int32, (1, 128), 1)
    for i in range(GROUP):
        row = g * GROUP + i
        lhs = jnp.concatenate(
            [acc[t, pl.ds(row, 32, stride=128), :] for t in range(2)], axis=1
        ).astype(BF16)
        res = lax.dot_general(
            lhs, leg_ref[i], (((1,), (1,)), ((), ())), preferred_element_type=F32
        )
        out_ref[pl.ds(i, 32, stride=GROUP), :] = jnp.where(degree >= order_ref[row], res, 0.0)


def latent_gradient(first_degree, orders_here, ret, leg):
    return pl.pallas_call(
        gradient_kernel,
        grid_spec=pltpu.PrefetchScalarGridSpec(
            num_scalar_prefetch=2,
            grid=(128 // GROUP,),
            in_specs=[
                pl.BlockSpec((4, 4, 32, 16, 128), lambda g, *_: (0, 0, 0, 0, 0)),
                pl.BlockSpec((GROUP, 128, 256), lambda g, *_: (g, 0, 0)),
            ],
            out_specs=pl.BlockSpec((None, 32 * GROUP, 128), lambda g, *_: (g, 0, 0)),
            scratch_shapes=[pltpu.VMEM((2, 4096, 128), F32)],
        ),
        out_shape=jax.ShapeDtypeStruct((128 // GROUP, 32 * GROUP, 128), F32),
        compiler_params=pltpu.CompilerParams(vmem_limit_bytes=40 * 2**20),
    )(first_degree, orders_here, ret, leg)


def sky_kernel(
    part, counts, weight, order_cols, t1, t4, w3, w3b, tw, twb, ret,
    in1, direct1, fwd_src, fwd1, y1, land2, spec_f, spec_b, spec_in,
    oh, oht, a1, zs, zb, xb, vb, ug, uc, un, rb, rr, fb, ga, tot_src, tot_in, tot2_src, tot2_in,
    send_sem, recv_sem,
):
    z, core = lax.axis_index("order_0"), lax.axis_index("order_1")
    x, y = lax.axis_index("blk_0"), lax.axis_index("blk_1")
    k = z * 2 + core
    b = x * 4 + y

    def order_peer(i):
        other = lax.rem(k + i, 16)
        return other, (other // 2, lax.rem(other, 2), x, y)

    def blk_peer(i):
        other = lax.rem(b + i, 16)
        return other, (z, core, other // 4, lax.rem(other, 4))

    def ring(h, i):
        if h == 0:
            return (z, core, lax.rem(x + i + 4, 4), y)
        return (z, core, x, lax.rem(y + i + 4, 4))

    barrier = pltpu.get_barrier_semaphore()
    for i in range(1, 16):
        pl.semaphore_signal(barrier, inc=1, device_id=order_peer(i)[1], device_id_type=MESH)
        pl.semaphore_signal(barrier, inc=1, device_id=blk_peer(i)[1], device_id_type=MESH)
    pl.semaphore_wait(barrier, 30)

    used = [0]
    started = []

    def send(src, dst, device):
        n = used[0]
        used[0] += 1
        copy = pltpu.make_async_remote_copy(
            src_ref=src,
            dst_ref=dst,
            send_sem=send_sem.at[n],
            recv_sem=recv_sem.at[n],
            device_id=device,
            device_id_type=MESH,
        )
        copy.start()
        started.append(copy)
        return copy

    def at(h, d, half):
        d = lax.rem(d + 4, 4)
        if h == 0:
            return part.at[d, pl.ds(2 * half, 2), pl.ds(0, 16)]
        return part.at[pl.ds(2 * half, 2), d, pl.ds(16, 16)]

    def load(h, d, half, row, pc):
        d = lax.rem(d + 4, 4)
        if h == 0:
            return part[d, 2 * half + row, pc].astype(F32)
        return part[2 * half + row, d, 16 + pc].astype(F32)

    q = (x, y)
    near, straight = {}, {}
    for h in range(2):
        for s, sign in enumerate((1, -1)):
            near[h, s] = send(at(h, q[h] + 2, s), in1.at[h, s], ring(h, sign))
    for h in range(2):
        for s, sign in enumerate((1, -1)):
            straight[h, s] = send(at(h, q[h] + sign, 1 - s), direct1.at[h, s], ring(h, sign))

    lane = lax.broadcasted_iota(jnp.int32, (128, 128), 1)
    sub = lax.broadcasted_iota(jnp.int32, (128, 128), 0)

    def build(i, _):
        cols = jnp.broadcast_to(order_cols[pl.ds(i, 1), :], (128, 128))
        rows = cols.T
        for t in range(16):
            value = 2.0
            value_t = 2.0
            if t == 0:
                value = jnp.where(lane == 0, 1.0, 2.0)
                value_t = jnp.where(sub == 0, 1.0, 2.0)
            base = 128 * t
            oh[i, :, 128 * t : 128 * t + 128] = jnp.where(rows == lane + base, value, 0.0).astype(BF16)
            oht[t, i] = jnp.where(cols == sub + base, value_t, 0.0).astype(BF16)
        return 0

    def relay(h, s, sign):
        near[h, s].wait_recv()

        def add(pc, _):
            for row in range(2):
                total = in1[h, s, row, pc].astype(F32) + load(h, q[h] + sign, s, row, pc)
                fwd_src[h, s, row, pc] = total.astype(BF16)
            return 0

        lax.fori_loop(0, 16, add, 0)
        return send(fwd_src.at[h, s], fwd1.at[h, s], ring(h, sign))

    def to_orders(out):
        for c in range(0, 16, 2):
            pair = jnp.concatenate(
                [xb[pl.ds(c + e, 32, stride=16), :] for e in range(2)], axis=1
            )
            ph, plo = hi_lo(pair)
            v = dot(w3b[...], jnp.concatenate([ph, ph, plo], axis=0))
            for e in range(2):
                re, im = v[:32, 128 * e : 128 * e + 128], v[32:, 128 * e : 128 * e + 128]
                co, si = twb[0:32, :], twb[32:64, :]
                turned = (re * co + im * si, im * co - re * si)
                for b2 in range(2):
                    for ri in range(2):
                        vb[2 * b2 + ri, pl.ds(c + e, 16, stride=16), :] = turned[ri][
                            16 * b2 : 16 * b2 + 16
                        ]
        lhs = jnp.concatenate([vb[i] for i in range(4)], axis=1)
        lh, ll = hi_lo(lhs)
        out[...] = dot(lh, t4[0:512, :]) + dot(lh, t4[512:1024, :]) + dot(ll, t4[0:512, :])

    count_sum = jnp.zeros((16, 128), F32)
    for j in range(32):
        tile = counts[:, 128 * j : 128 * j + 128].astype(F32)
        xb[16 * j : 16 * j + 16, :] = tile
        count_sum = count_sum + tile
    to_orders(uc)

    passed = {}
    for h in range(2):
        for s, sign in enumerate((1, -1)):
            passed[h, s] = relay(h, s, sign)

    lax.fori_loop(0, 16, build, 0)

    second = {}
    for h in range(2):
        for s in range(2):
            straight[h, s].wait_recv()
            passed[h, s].wait_recv()

        def add(pc, _):
            for half in range(2):
                for row in range(2):
                    total = (
                        load(h, q[h], half, row, pc)
                        + fwd1[h, half, row, pc].astype(F32)
                        + direct1[h, 1 - half, row, pc].astype(F32)
                    )
                    y1[h, 2 * half + row, pc] = total.astype(BF16)
            return 0

        lax.fori_loop(0, 16, add, 0)
        for i in range(1, 4):
            d = lax.rem(q[1 - h] + i, 4)
            second[h, i] = send(y1.at[h, d], land2.at[h, i - 1], ring(1 - h, i))
    for h in range(2):
        for i in range(1, 4):
            second[h, i].wait_recv()

        def add(pc, _):
            total = y1[h, q[1 - h], pc].astype(F32)
            for i in range(3):
                total = total + land2[h, i, pc].astype(F32)
            spec_f[pl.ds(16 * h + pc, 16, stride=32), :] = total
            return 0

        lax.fori_loop(0, 16, add, 0)
    spec_b[...] = spec_f[...].astype(BF16).reshape(16, 32, 128)

    moved = {}
    for i in range(1, 16):
        other, device = order_peer(i)
        moved[i] = send(spec_b.at[other], spec_in.at[k], device)
    spec_in[k] = spec_b[k]
    for i in range(1, 16):
        moved[i].wait_recv()

    lhs = jnp.concatenate([spec_in[i] for i in range(16)], axis=1)
    for t in range(8):
        rhs = jnp.concatenate([oh[i, :, 256 * t : 256 * t + 256] for i in range(16)], axis=0)
        tile = dot(lhs, rhs).astype(BF16)
        for e in range(2):
            a1[32 * (2 * t + e) : 32 * (2 * t + e) + 32, :] = tile[:, 128 * e : 128 * e + 128]
    twice = jnp.concatenate([a1[...], a1[...]], axis=1)
    zs[...] = dot(twice, t1[...])
    for b1 in range(16):
        for b2 in range(2):
            bb = 2 * b1 + b2
            top, bottom = 32 * b1, 32 * b1 + 16
            c0 = zs[top : top + 16, 256 * b2 : 256 * b2 + 128]
            d0 = zs[top : top + 16, 256 * b2 + 128 : 256 * b2 + 256]
            c1 = zs[bottom : bottom + 16, 256 * b2 : 256 * b2 + 128]
            d1 = zs[bottom : bottom + 16, 256 * b2 + 128 : 256 * b2 + 256]
            re, im = c0 - d1, d0 + c1
            co, si = tw[bb : bb + 1, :], tw[32 + bb : 33 + bb, :]
            zb[pl.ds(bb, 16, stride=64), :] = re * co - im * si
            zb[pl.ds(32 + bb, 16, stride=64), :] = re * si + im * co
    for c in range(0, 16, 2):
        pair = jnp.concatenate([zb[64 * (c + e) : 64 * (c + e) + 64, :] for e in range(2)], axis=1)
        ph, plo = hi_lo(pair)
        m = dot(w3[...], jnp.concatenate([ph, ph, plo], axis=0))
        for e in range(2):
            xb[pl.ds(c + e, 32, stride=16), :] = m[:, 128 * e : 128 * e + 128]
    growth_sum = jnp.zeros((16, 128), F32)
    for j in range(32):
        tile = weight[:, 128 * j : 128 * j + 128] * jnp.exp(xb[16 * j : 16 * j + 16, :])
        xb[16 * j : 16 * j + 16, :] = tile
        growth_sum = growth_sum + tile

    chain = lax.broadcasted_iota(jnp.int32, (16, 128), 0)
    lane16 = lax.broadcasted_iota(jnp.int32, (16, 128), 1)
    row = jnp.where(lane16 == chain, jnp.sum(growth_sum, axis=1, keepdims=True), 0.0) + jnp.where(
        lane16 == chain + 16, jnp.sum(count_sum, axis=1, keepdims=True), 0.0
    )
    row = jnp.sum(row, axis=0, keepdims=True)
    tot_src[...] = jnp.broadcast_to(row, (8, 128))
    sums = {}
    for i in range(1, 16):
        sums[i] = send(tot_src, tot_in.at[i - 1], order_peer(i)[1])
    to_orders(ug)
    total = tot_src[...]
    for i in range(1, 16):
        sums[i].wait_recv()
        total = total + tot_in[i - 1]
    tot2_src[...] = total
    for i in range(1, 16):
        sums[i] = send(tot2_src, tot2_in.at[i - 1], blk_peer(i)[1])
    for i in range(1, 16):
        sums[i].wait_recv()
        total = total + tot2_in[i - 1]
    row = jnp.broadcast_to(total[0:1, :], (16, 128))
    total_growth = jnp.sum(jnp.where(lane16 == chain, row, 0.0), axis=1, keepdims=True)
    total_counts = jnp.sum(jnp.where(lane16 == chain + 16, row, 0.0), axis=1, keepdims=True)
    ratio = jnp.broadcast_to(total_counts / total_growth, (16, 256))

    for b1 in range(16):
        rows = slice(16 * b1, 16 * b1 + 16)
        u = (ug[rows, :] * ratio - uc[rows, :]) * (1.0 / 64.0)
        un[:, 128 * b1 : 128 * b1 + 128] = jnp.concatenate([u[:, :128], u[:, 128:]], axis=0).astype(BF16)
    for i in range(0, 16, 2):
        rhs = jnp.concatenate(
            [jnp.concatenate([oht[t, i + e] for t in range(16)], axis=0) for e in range(2)], axis=1
        )
        r = dot(un[...], rhs).astype(BF16)
        for e in range(2):
            rb[i + e] = r[:, 128 * e : 128 * e + 128]
    for i in range(1, 16):
        other, device = order_peer(i)
        moved[i] = send(rb.at[other], rr.at[k], device)
    rr[k] = rb[k]
    for i in range(1, 16):
        moved[i].wait_recv()
    for i in range(16):
        fb[pl.ds(i, 32, stride=16), :] = rr[i].astype(F32)
    ga[x, y] = fb[...].astype(BF16).reshape(32, 16, 128)

    def own(h):
        return ga.at[x, y, pl.ds(16 * h, 16)]

    first = {}
    for h in range(2):
        for i in range(1, 4):
            first[h, i] = send(own(h), own(h), ring(1 - h, i))

    def group(h, d, half):
        d = lax.rem(d + 4, 4)
        if h == 0:
            return ga.at[d, pl.ds(2 * half, 2), pl.ds(0, 16)]
        return ga.at[pl.ds(2 * half, 2), d, pl.ds(16, 16)]

    for h in range(2):
        for i in range(1, 4):
            first[h, i].wait_recv()
        for s, sign in enumerate((1, -1)):
            near[h, s] = send(group(h, q[h], s), group(h, q[h], s), ring(h, sign))
        for s, sign in enumerate((1, -1)):
            straight[h, s] = send(group(h, q[h], 1 - s), group(h, q[h], 1 - s), ring(h, sign))
    for h in range(2):
        for s, sign in enumerate((1, -1)):
            near[h, s].wait_recv()
            piece = group(h, q[h] - sign, s)
            passed[h, s] = send(piece, piece, ring(h, sign))
    for h in range(2):
        for s in range(2):
            straight[h, s].wait_recv()
            passed[h, s].wait_recv()
    for copy in started:
        copy.wait_send()
    ret[...] = ga[...]


N_SENDS = 12 + 6 + 15 + 30 + 15 + 6 + 12


def sky(part, counts, weight, order_cols):
    t = [jnp.asarray(a) for a in tables()]
    vm = pltpu.VMEM
    return pl.pallas_call(
        sky_kernel,
        out_shape=jax.ShapeDtypeStruct((4, 4, 32, 16, 128), BF16),
        in_specs=[pl.BlockSpec(memory_space=pltpu.VMEM)] * (4 + len(t)),
        out_specs=pl.BlockSpec(memory_space=pltpu.VMEM),
        scratch_shapes=[
            vm((2, 2, 2, 16, 16, 128), BF16),
            vm((2, 2, 2, 16, 16, 128), BF16),
            vm((2, 2, 2, 16, 16, 128), BF16),
            vm((2, 2, 2, 16, 16, 128), BF16),
            vm((2, 4, 16, 16, 128), BF16),
            vm((2, 3, 16, 16, 128), BF16),
            vm((512, 128), F32),
            vm((16, 32, 128), BF16),
            vm((16, 32, 128), BF16),
            vm((16, 128, 2048), BF16),
            vm((16, 16, 128, 128), BF16),
            vm((512, 128), BF16),
            vm((512, 512), F32),
            vm((1024, 128), F32),
            vm((512, 128), F32),
            vm((4, 256, 128), F32),
            vm((256, 256), F32),
            vm((256, 256), F32),
            vm((32, 2048), BF16),
            vm((16, 32, 128), BF16),
            vm((16, 32, 128), BF16),
            vm((512, 128), F32),
            vm((4, 4, 32, 16, 128), BF16),
            vm((8, 128), F32),
            vm((15, 8, 128), F32),
            vm((8, 128), F32),
            vm((15, 8, 128), F32),
            pltpu.SemaphoreType.DMA((N_SENDS,)),
            pltpu.SemaphoreType.DMA((N_SENDS,)),
        ],
        compiler_params=pltpu.CompilerParams(
            collective_id=0, has_side_effects=True, vmem_limit_bytes=58 * 2**20
        ),
    )(part, counts, weight, order_cols, *t)


def body(latent, legendre, counts, exposure, slot_order):
    slot_count, degrees, cycle_count = legendre.shape
    orders_here = lax.dynamic_slice_in_dim(
        slot_order, lax.axis_index(ORDER) * slot_count, slot_count
    )
    first_degree = lax.axis_index(BLK) * degrees
    degree = first_degree + lax.iota(jnp.int32, degrees)
    nonzero = degree[None, :] >= orders_here[:, None]
    masked = jnp.where(nonzero[None, None], latent, jnp.zeros((), latent.dtype))
    lat = jnp.transpose(masked.reshape(32, slot_count, degrees), (1, 0, 2))
    part = partial_spectra(lat, legendre)
    cycle = lax.axis_index(BLK) * lax.axis_size(ORDER) + lax.axis_index(ORDER)
    cycle_area = jnp.sin(jnp.pi * (cycle.astype(F32) + 0.5) / 256)
    weight = cycle_area * exposure
    order_cols = (lax.rem(slot_order, 32) * 64 + slot_order // 32).reshape(16, 128)
    ret = sky(part, counts[0], weight, order_cols)
    grad = latent_gradient(first_degree[None], orders_here, ret, legendre)
    grad = grad.reshape(128 // GROUP, 32, GROUP, 128).transpose(1, 0, 2, 3)
    return grad.reshape(2, 16, slot_count, degrees)


def solution(mesh):
    finer = Mesh(mesh.devices.reshape(8, 2, 4, 4), AXES)
    return jax.shard_map(
        body,
        mesh=finer,
        in_specs=(
            P(None, None, ORDER, BLK),
            P(ORDER, BLK, None),
            P(BLK_ORDER, None, None),
            P(BLK_ORDER, None),
            P(),
        ),
        out_specs=P(None, None, ORDER, BLK),
        check_vma=False,
    )
```

time: 306 us -> 105 us (0.34)
  waiting for transfers between devices: 170 us -> 0 us
  Pallas kernels: 0 us -> 87.8 us
  blocking collectives: 70.3 us -> 0 us
  matrix products: 23.9 us -> 0 us
  between operations: 13.3 us -> 0.15 us
  other arithmetic: 14.9 us -> 4 us
    reduce_scatter x3 -> x0, waiting for transfers between devices: 131 us -> none  [the longest x2 70.6 us: own_rows(): subtotal = lax.psum_scatter(subtotal, axis, scatter_dimension=0, tiled=True)]
    pallas_call x0 -> x3, Pallas kernels: none -> 87.9 us  [the longest x1 72.5 us: sky(): pl.pallas_call(sky_kernel, out_shape=jax.ShapeDtypeStruct((4, 4, 32, 16,...]
    all_gather x1 -> x0, waiting for transfers between devices: 38.5 us -> none  [work_in_pieces(): blocks = [lax.all_gather(share, axis) for share in pieces]]
    psum x4 -> x0, blocking collectives: 36.8 us -> none  [by_axis(): return functools.reduce(lax.psum, axes, array)]
    all_to_all x1 -> x0, blocking collectives: 33.5 us -> none  [from_everyone(): return lax.all_to_all(copies, axis, split_axis=0, concat_axis=0, tiled=True)]
    dot_general x4 -> x0, matrix products: 23.9 us -> none  [the longest x1 6.98 us: body(): jnp.einsum('rpcs,slr->pcsl', gathered_copies(returned, BLK, 0), basis, pr...]
    unnamed x4 -> x8, local copies, waits for them, and re-layouts: 0.79 us -> 9.66 us
    mul x2 -> x1, other arithmetic: 9.76 us -> 1.33 us  [body(): weight = cycle_area * exposure]
  transfers between devices with their start and end apart: 4 -> 0, of which waited for: 4 -> 0; matrix products, arithmetic and copies ran while one was open for 3% -> 0% of each run, Pallas kernels for 0% -> 0%
where the time goes in v1:
time: 105 us
  Pallas kernels  87.8 us (84%)
  local copies, waits for them, and re-layouts  12.7 us (12%)
  other arithmetic  4 us (4%)
    pallas_call x1, Pallas kernels, sky(): pl.pallas_call(sky_kernel, out_shape=jax.ShapeDtypeStruct((4, 4, 32, 16,...  72.5 us
    unnamed x8, local copies, waits for them, and re-layouts  9.66 us
    pallas_call x1, Pallas kernels, latent_gradient(): pl.pallas_call(gradient_kernel, grid_spec=pltpu.PrefetchScalarGridSpec(nu...  7.86 us
    pallas_call x1, Pallas kernels, partial_spectra(): pl.pallas_call(spectra_kernel, grid=(128 // GROUP,), out_shape=jax.ShapeD...  7.48 us

profile of v1, /device:TPU:1, one launch (start us, length us, event | category | flops | bytes accessed | tf_op | source)
XLA Modules:
  0.0 104.7 jit_solution(17991068249401227212)
XLA Ops:
  0.1 0.8 dynamic_slice.3.order_ref
  0.9 1.3 %fusion.1.order_cols = s32[16,128]{1,0:T(8,128)} fusion(s32[2048]{0:T(1024)} %param.15), kind=kLoop, calls=%fused_computation.7 | loop fusion | flops 34816 | bytes 16384 | tf_op jit(solution)/shard_map/reshape | solution.py:506
  2.1 0.1 broadcast_compare_fusion
  2.2 1.3 %broadcast_multiply_fusion.weight = f32[1,4096]{1,0:T(1,128)} fusion(f32[1,4096]{1,0:T(1,128)} %param.14, f32[]{:T(128)S(6)} %sin.3), kind=kLoop, calls=%fused_computation.10 | loop fusion | flops 4096 | bytes 32772 | tf_op jit(solution)/shard_map/mul | solution.py:505
  3.6 1.3 %broadcast_select_fusion = bf16[2,16,128,128]{3,2,1,0:T(8,128)(2,1)S(1)} fusion(bf16[2,16,128,128]{3,2,1,0:T(8,128)(2,1)} %param.11, pred[128,128]{1,0:T(8,128)(4,1)S(1)} %broadcast_compare_fusion), kind=kLoop, calls=%fused_computation | loop fusion | flops 524288 | bytes 2113536 | tf_op jit(solution)/shard_map/jit(_where)/select_n | solution.py:500
  4.9 0.7 copy.12
  5.5 0.0 copy-start
  5.6 3.4 %copy-done = bf16[128,128,256]{2,1,0:T(8,128)(2,1)S(1)} copy-done((bf16[128,128,256]{2,1,0:T(8,128)(2,1)S(1)}, bf16[128,128,256]{2,1,0:T(8,128)(2,1)}, u32[]{:S(2)}) %copy-start) | copy-done | bytes 8388632
  8.9 7.5 %shard_map.109.part = bf16[4,4,32,16,128]{4,3,2,1,0:T(8,128)(2,1)S(1)} custom-call(bf16[128,32,128]{2,1,0:T(8,128)(2,1)S(1)} %bitcast.12, bf16[128,128,256]{2,1,0:T(8,128)(2,1)S(1)} %copy-done), custom_call_target="tpu_custom_call" | custom-call | tf_op jit(solution)/shard_map/pallas_call | solution.py:97
  16.4 0.0 copy-start.3
  16.4 1.3 %copy-done.3 = bf16[4,4,32,16,128]{4,3,2,1,0:T(8,128)(2,1)} copy-done((bf16[4,4,32,16,128]{4,3,2,1,0:T(8,128)(2,1)}, bf16[4,4,32,16,128]{4,3,2,1,0:T(8,128)(2,1)S(1)}, u32[]{:S(2)}) %copy-start.3) | copy-done | bytes 2097176
  17.7 72.5 %shard_map.110.ret_ref = bf16[4,4,32,16,128]{4,3,2,1,0:T(8,128)(2,1)} custom-call(bf16[4,4,32,16,128]{4,3,2,1,0:T(8,128)(2,1)} %copy-done.3, s32[16,4096]{1,0:T(8,128)} %bitcast.13, f32[1,4096]{1,0:T(1,128)} %broadcast_multiply_fusion.weight, s32[16,128]{1,0:T(8,128)} %fusion.1.order_cols, bf16[256,512]{1,0:T(8,128)(2,1)} %constant.70.clone.t1, ...), custom_call_target="tpu_custom_call" | custom-call | tf_op jit(solution)/shard_map/pallas_call | solution.py:450
  90.3 0.0 copy-start.1
  90.3 3.4 %copy-done.1 = bf16[128,128,256]{2,1,0:T(8,128)(2,1)S(1)} copy-done((bf16[128,128,256]{2,1,0:T(8,128)(2,1)S(1)}, bf16[128,128,256]{2,1,0:T(8,128)(2,1)}, u32[]{:S(2)}) %copy-start.1) | copy-done | bytes 8388632
  93.6 0.0 copy-start.2
  93.6 1.6 %copy-done.2 = bf16[4,4,32,16,128]{4,3,2,1,0:T(8,128)(2,1)S(1)} copy-done((bf16[4,4,32,16,128]{4,3,2,1,0:T(8,128)(2,1)S(1)}, bf16[4,4,32,16,128]{4,3,2,1,0:T(8,128)(2,1)}, u32[]{:S(2)}) %copy-start.2) | copy-done | bytes 2097176
  95.2 7.9 %shard_map.111 = f32[8,512,128]{2,1,0:T(8,128)S(1)} custom-call(s32[1]{0:T(128)} %bitcast.first_degree_ref, s32[128]{0:T(128)S(1)} %dynamic_slice.3.order_ref, bf16[4,4,32,16,128]{4,3,2,1,0:T(8,128)(2,1)S(1)} %copy-done.2, bf16[128,128,256]{2,1,0:T(8,128)(2,1)S(1)} %copy-done.1), custom_call_target="tpu_custom_call" | custom-call | tf_op jit(solution)/shard_map/pallas_call | solution.py:138
  103.1 1.6 %copy.13 = f32[32,8,16,128]{3,2,1,0:T(8,128)} copy(f32[32,8,16,128]{3,2,0,1:T(8,128)S(1)} %bitcast.11) | data formatting | bytes 4194304 | tf_op jit(solution)/shard_map/transpose | solution.py:509
  (1 shorter events, 0.0 us)
Async XLA Ops:
  5.5 3.4 %copy-start = (bf16[128,128,256]{2,1,0:T(8,128)(2,1)S(1)}, bf16[128,128,256]{2,1,0:T(8,128)(2,1)}, u32[]{:S(2)}) copy-start(bf16[128,128,256]{2,1,0:T(8,128)(2,1)} %leg_ref.3) | copy-start | bytes 25165828
  16.4 1.3 %copy-start.3 = (bf16[4,4,32,16,128]{4,3,2,1,0:T(8,128)(2,1)}, bf16[4,4,32,16,128]{4,3,2,1,0:T(8,128)(2,1)S(1)}, u32[]{:S(2)}) copy-start(bf16[4,4,32,16,128]{4,3,2,1,0:T(8,128)(2,1)S(1)} %shard_map.109.part) | copy-start | bytes 6291460
  90.3 3.4 %copy-start.1 = (bf16[128,128,256]{2,1,0:T(8,128)(2,1)S(1)}, bf16[128,128,256]{2,1,0:T(8,128)(2,1)}, u32[]{:S(2)}) copy-start(bf16[128,128,256]{2,1,0:T(8,128)(2,1)} %leg_ref.3) | copy-start | bytes 25165828
  93.6 1.6 %copy-start.2 = (bf16[4,4,32,16,128]{4,3,2,1,0:T(8,128)(2,1)S(1)}, bf16[4,4,32,16,128]{4,3,2,1,0:T(8,128)(2,1)}, u32[]{:S(2)}) copy-start(bf16[4,4,32,16,128]{4,3,2,1,0:T(8,128)(2,1)} %shard_map.110.ret_ref) | copy-start | bytes 6291460
